TPU v7x, 32 devices: a whole 2x2x4 slice. The times are simulated.
32 devices in a mesh: sweep: 2 (over y), row: 4 (over x, core), col: 4 (over z).
Axes of the slice: x: 2, y: 2, z: 4, core: 2. Of those that a mesh axis runs over, the one named last changes fastest.
Arguments:
- tokens: bfloat16 [160, 4096], P(('sweep', 'col'), 'row'), parts along dimension 0, may hold values from -6 to 6
- w_gate: bfloat16 [4096, 14336], P('row', 'col'), may hold values from -0.09375 to 0.09375
- w_up: bfloat16 [4096, 14336], P('row', 'col'), may hold values from -0.09375 to 0.09375
- w_down: bfloat16 [14336, 4096], P('col', 'row'), may hold values from -0.046875 to 0.046875
- cotangent: bfloat16 [160, 4096], P(('sweep', 'col'), 'row'), parts along dimension 0, may hold values from -6 to 6
- step_rate: float32 [2], P('sweep'), parts along dimension 0, may hold values from 0.05 to 0.3
Outputs:
- out_rows: bfloat16 [160, 4096], P(('sweep', 'col'), 'row'), parts along dimension 0
- grad_in: bfloat16 [160, 4096], P(('sweep', 'col'), 'row'), parts along dimension 0
- step_gate: bfloat16 [8192, 14336], P(('sweep', 'row'), 'col'), parts along dimension 0
- step_up: bfloat16 [8192, 14336], P(('sweep', 'row'), 'col'), parts along dimension 0
- step_down: bfloat16 [28672, 4096], P(('sweep', 'col'), 'row'), parts along dimension 0
There are 2 independent parts, one for each index of `sweep`. A program takes and returns all parts, laid end to end along the dimension named above; an argument that names none is the same for every part. Nothing has to cross between parts.
All inputs are finite; a program needn't handle non-finite values.
Results may differ from a plain program's by a relative error of at most 0.0049.
Values may be sent and summed in bfloat16 or wider, within the bound.
A program may use at most 128 MiB of HBM per device.

v0:
```python
import jax
import jax.numpy as jnp
from jax import lax
from jax.sharding import PartitionSpec as P


def swiglu_back(back_hidden, gate_val, up_val):
    gate_sig = jax.nn.sigmoid(gate_val)
    activation = gate_val * gate_sig
    back_gate = (back_hidden * up_val * gate_sig * (1.0 + gate_val * (1.0 - gate_sig))).astype(
        jnp.bfloat16
    )
    back_up = (back_hidden * activation).astype(jnp.bfloat16)
    return (back_gate, back_up)


def forward_hidden(gate_val, up_val):
    gate_sig = jax.nn.sigmoid(gate_val)
    return (gate_val * gate_sig * up_val).astype(jnp.bfloat16)


def contract_last(left, right):
    return lax.dot_general(
        left, right, (((1,), (1,)), ((), ())), preferred_element_type=jnp.float32
    )


def contract_first(left, right):
    return lax.dot_general(
        left, right, (((0,), (0,)), ((), ())), preferred_element_type=jnp.float32
    )


def local(tokens, w_gate, w_up, w_down, cotangent, step_rate):
    tokens_all = lax.all_gather(tokens, "col", axis=0, tiled=True)
    hidden_width = w_gate.shape[1]
    w_both = jnp.concatenate([w_gate, w_up], axis=1)
    picked = tokens_all
    summed = lax.psum_scatter(
        jnp.dot(picked, w_both, preferred_element_type=jnp.float32),
        "row",
        scatter_dimension=0,
        tiled=True,
    )
    gate_val = summed[:, :hidden_width]
    up_val = summed[:, hidden_width:]
    hidden = forward_hidden(gate_val, up_val)
    hidden_all = lax.all_gather(hidden, "row", axis=0, tiled=True)
    picked = hidden_all
    branch_out = lax.psum_scatter(
        jnp.dot(picked, w_down, preferred_element_type=jnp.float32),
        "col",
        scatter_dimension=0,
        tiled=True,
    )
    out_rows = (tokens.astype(jnp.float32) + branch_out).astype(jnp.bfloat16)
    cotangent_all = lax.all_gather(cotangent, "col", axis=0, tiled=True)
    picked = cotangent_all
    back_hidden = lax.psum_scatter(
        contract_last(picked, w_down), "row", scatter_dimension=0, tiled=True
    )
    back_gate, back_up = swiglu_back(back_hidden, gate_val, up_val)
    gate_grad_all, up_grad_all = (
        lax.all_gather(back_gate, "row", axis=0, tiled=True),
        lax.all_gather(back_up, "row", axis=0, tiled=True),
    )
    grads_all = jnp.concatenate([gate_grad_all, up_grad_all], axis=1)
    picked = grads_all
    input_sums = lax.psum_scatter(
        contract_last(picked, w_both), "col", scatter_dimension=0, tiled=True
    )
    grad_in = (cotangent.astype(jnp.float32) + input_sums).astype(jnp.bfloat16)
    factor = -step_rate[0]
    weight_grads = contract_first(tokens_all, grads_all)
    step_gate = (factor * weight_grads[:, :hidden_width]).astype(jnp.bfloat16)
    step_up = (factor * weight_grads[:, hidden_width:]).astype(jnp.bfloat16)
    step_down = (factor * contract_first(hidden_all, cotangent_all)).astype(jnp.bfloat16)
    return (out_rows, grad_in, step_gate, step_up, step_down)


def solution(mesh):
    in_specs = (
        P(("sweep", "col"), "row"),
        P("row", "col"),
        P("row", "col"),
        P("col", "row"),
        P(("sweep", "col"), "row"),
        P("sweep"),
    )
    out_specs = (
        P(("sweep", "col"), "row"),
        P(("sweep", "col"), "row"),
        P(("sweep", "row"), "col"),
        P(("sweep", "row"), "col"),
        P(("sweep", "col"), "row"),
    )
    return jax.shard_map(local, mesh=mesh, in_specs=in_specs, out_specs=out_specs, check_vma=False)
```

profile of v0, /device:TPU:0, one launch (start us, length us, event | category | flops | bytes accessed | tf_op | source)
XLA Modules:
  0.0 232.2 jit_solution(10670757781399332932)
XLA Ops:
  7.2 0.0 copy-start.1
  7.2 0.0 all-reduce.10.cloned.1.call-start
  7.2 6.6 %constant_dynamic-update-slice_fusion.1 = bf16[1024,7168]{1,0:T(8,128)(2,1)} fusion(bf16[1024,3584]{1,0:T(8,128)(2,1)} %param.7), kind=kLoop, calls=%fused_computation.20 | loop fusion | bytes 14680064
  13.8 0.0 copy-done.1
  13.8 15.5 %all-gather = bf16[4,20,1024]{2,1,0:T(8,128)(2,1)S(1)} all-gather(bf16[1,20,1024]{2,1,0:T(8,128)(2,1)S(1)} %bitcast.35), channel_id=1, replica_groups=mesh['sweep'=2,'row'=4,'col'=4] {'col'}, dimensions={0}, use_global_device_ids=true | all-gather | bytes 204800 | tf_op jit(solution)/shard_map/all_gather | solution.py:35
  29.3 6.5 %constant_dynamic-update-slice_fusion = bf16[1024,7168]{1,0:T(8,128)(2,1)} fusion(bf16[1024,7168]{1,0:T(8,128)(2,1)} %constant_dynamic-update-slice_fusion.1, bf16[1024,3584]{1,0:T(8,128)(2,1)} %param.8), kind=kLoop, calls=%fused_computation.19 | loop fusion | bytes 14680064 | tf_op jit(solution)/shard_map/concatenate | solution.py:37
  35.8 0.0 copy-start
  35.8 9.2 %convolution_bitcast_fusion.1 = f32[80,7168]{1,0:T(8,128)} fusion(bf16[80,1024]{1,0:T(8,128)(2,1)S(1)} %reshape.12, bf16[1024,7168]{1,0:T(8,128)(2,1)} %constant_dynamic-update-slice_fusion), kind=kOutput, calls=%fused_computation.6 | convolution fusion | flops 1174405120 | bytes 17137664 | tf_op jit(solution)/shard_map/dot_general | solution.py:40
  45.0 0.0 copy-start.3
  45.0 0.0 copy-start.2
  45.0 0.0 all-reduce.10.cloned.1.call-update
  45.1 0.0 copy-done
  45.1 14.0 %all-gather.2 = bf16[4,20,1024]{2,1,0:T(8,128)(2,1)S(1)} all-gather(bf16[1,20,1024]{2,1,0:T(8,128)(2,1)S(1)} %bitcast.34), channel_id=1, replica_groups=mesh['sweep'=2,'row'=4,'col'=4] {'col'}, dimensions={0}, use_global_device_ids=true | all-gather | bytes 204800 | tf_op jit(solution)/shard_map/all_gather | solution.py:57
  59.1 5.5 %fusion.14 = f32[80,3584]{1,0:T(8,128)S(1)} fusion(bf16[80,1024]{1,0:T(8,128)(2,1)S(1)} %reshape.16, bf16[3584,1024]{1,0:T(8,128)(2,1)} %param.9), kind=kOutput, calls=%fused_computation.25 | convolution fusion | flops 587202560 | bytes 8650752 | tf_op jit(solution)/shard_map/dot_general | solution.py:23
  64.6 18.8 %fusion.1 = f32[24,3584]{1,0:T(8,128)S(1)} fusion(f32[80,3584]{1,0:T(8,128)S(1)} %fusion.14), kind=kCustom, calls=%all-reduce-scatter.1 | all-reduce-scatter fusion | flops 344065 | bytes 1491456
  83.5 1.3 collective-permute-start.1
  84.8 0.0 copy-done.3
  84.8 0.6 dynamic-slice.12
  85.4 0.0 copy-done.2
  85.4 0.6 fusion.12
  88.6 0.0 collective-permute-done.1
  88.6 0.4 concatenate.9
  89.0 16.1 %all-reduce.10.cloned.1.call-done = f32[80,7168]{1,0:T(8,128)} async-done(((f32[80,7168]{1,0:T(8,128)}), f32[80,7168]{1,0:T(8,128)}) %all-reduce.10.cloned.1.call-update) | async-done | bytes 2293776
  105.0 1.4 fusion.7
  106.5 9.3 %all-gather.3 = bf16[4,20,3584]{2,1,0:T(8,128)(2,1)S(1)} all-gather(bf16[1,20,3584]{2,1,0:T(8,128)(2,1)S(1)} %get-tuple-element.27), channel_id=1, replica_groups=mesh['sweep'=2,'row'=4,'col'=4] {'row'}, dimensions={0}, use_global_device_ids=true | all-gather | bytes 716800 | tf_op jit(solution)/shard_map/all_gather | solution.py:64
  115.7 0.1 reshape.18
  115.9 8.4 %all-gather.4 = bf16[4,20,3584]{2,1,0:T(8,128)(2,1)S(1)} all-gather(bf16[1,20,3584]{2,1,0:T(8,128)(2,1)S(1)} %get-tuple-element.26), channel_id=1, replica_groups=mesh['sweep'=2,'row'=4,'col'=4] {'row'}, dimensions={0}, use_global_device_ids=true | all-gather | bytes 716800 | tf_op jit(solution)/shard_map/all_gather | solution.py:65
  124.3 0.1 reshape.20
  124.4 9.7 %fusion.15 = f32[80,1024]{1,0:T(8,128)S(1)} fusion(bf16[80,7168]{1,0:T(8,128)(2,1)S(1)} %constant_dynamic-update-slice_fusion.2, bf16[1024,7168]{1,0:T(8,128)(2,1)} %constant_dynamic-update-slice_fusion), kind=kOutput, calls=%fused_computation.26 | convolution fusion | flops 1174405120 | bytes 16154624 | tf_op jit(solution)/shard_map/dot_general | solution.py:23
  134.2 11.7 %convolution_bitcast_fusion = f32[1024,7168]{0,1:T(8,128)} fusion(bf16[80,7168]{1,0:T(8,128)(2,1)S(1)} %constant_dynamic-update-slice_fusion.2, bf16[80,1024]{1,0:T(8,128)(2,1)S(1)} %reshape.12), kind=kOutput, calls=%fused_computation | convolution fusion | flops 1174405120 | bytes 30670848 | tf_op jit(solution)/shard_map/dot_general | solution.py:29
  145.8 8.1 %all-gather.1 = bf16[4,20,3584]{2,1,0:T(8,128)(2,1)S(1)} all-gather(bf16[1,20,3584]{2,1,0:T(8,128)(2,1)S(1)} %get-tuple-element.28), channel_id=1, replica_groups=mesh['sweep'=2,'row'=4,'col'=4] {'row'}, dimensions={0}, use_global_device_ids=true | all-gather | bytes 716800 | tf_op jit(solution)/shard_map/all_gather | solution.py:48
  154.0 0.1 reshape.14
  154.1 4.5 %fusion.13 = f32[80,1024]{1,0:T(8,128)S(1)} fusion(bf16[80,3584]{1,0:T(8,128)(2,1)S(1)} %reshape.14, bf16[3584,1024]{1,0:T(8,128)(2,1)} %param.9), kind=kOutput, calls=%fused_computation.24 | convolution fusion | flops 587202560 | bytes 8241152 | tf_op jit(solution)/shard_map/dot_general | solution.py:51
  158.6 21.7 %fusion.11 = (f32[24,1024]{1,0:T(8,128)S(1)}, f32[24,1024]{1,0:T(8,128)S(1)}) fusion(f32[80,1024]{1,0:T(8,128)S(1)} %fusion.13, f32[80,1024]{1,0:T(8,128)S(1)} %fusion.15), kind=kCustom, calls=%all-reduce-scatter.3 | all-reduce-scatter fusion | flops 196609 | bytes 852480
  180.3 1.4 collective-permute-start.2
  181.8 1.9 collective-permute-start
  183.7 5.2 %multiply_convert_fusion = bf16[3584,1024]{1,0:T(8,128)(2,1)} fusion(bf16[80,3584]{1,0:T(8,128)(2,1)S(1)} %reshape.14, bf16[80,1024]{1,0:T(8,128)(2,1)S(1)} %reshape.16, f32[]{:T(128)} %bitcast.6), kind=kOutput, calls=%fused_computation.5 | convolution fusion | flops 594542592 | bytes 8077316 | tf_op jit(solution)/shard_map/dot_general | solution.py:29
  188.8 15.1 %fusion.3 = (bf16[1024,3584]{0,1:T(8,128)(2,1)}, bf16[1024,3584]{0,1:T(8,128)(2,1)}) fusion(f32[1024,7168]{0,1:T(8,128)} %convolution_bitcast_fusion, f32[]{:T(128)} %bitcast.6), kind=kLoop, calls=%fused_computation.2 | loop fusion | flops 14680064 | bytes 44040196 | tf_op jit(solution)/shard_map/convert_element_type | solution.py:76
  203.9 9.9 %copy.15 = bf16[1024,3584]{1,0:T(8,128)(2,1)} copy(bf16[1024,3584]{0,1:T(8,128)(2,1)} %get-tuple-element.25) | data formatting | bytes 14680064
  213.8 9.9 %copy.16 = bf16[1024,3584]{1,0:T(8,128)(2,1)} copy(bf16[1024,3584]{0,1:T(8,128)(2,1)} %get-tuple-element.24) | data formatting | bytes 14680064
  223.8 0.0 collective-permute-done.2
  223.8 0.2 concatenate.10
  223.9 0.6 fusion.9
  224.6 0.0 collective-permute-done
  224.6 0.2 concatenate.8
  224.7 0.6 fusion.10
  (7 shorter events, 0.2 us)
Async XLA Ops:
  7.2 6.6 %copy-start.1 = (bf16[20,1024]{1,0:T(8,128)(2,1)S(1)}, bf16[20,1024]{1,0:T(8,128)(2,1)}, u32[]{:S(2)}) copy-start(bf16[20,1024]{1,0:T(8,128)(2,1)} %param.6) | copy-start | bytes 122884
  7.2 97.9 %all-reduce.10.cloned.1.call-start = ((), (), s32[]{:S(2)}) async-start(), calls=%async_computation | async-start | bytes 4587520
  35.8 9.2 %copy-start = (bf16[20,1024]{1,0:T(8,128)(2,1)S(1)}, bf16[20,1024]{1,0:T(8,128)(2,1)}, u32[]{:S(2)}) copy-start(bf16[20,1024]{1,0:T(8,128)(2,1)} %param.10) | copy-start | bytes 122884
  45.0 39.8 %copy-start.3 = (u32[32]{0:T(128)S(1)}, u32[32]{0:T(128)}, u32[]{:S(2)}) copy-start(u32[32]{0:T(128)} %constant.11) | copy-start | bytes 388
  45.0 40.4 %copy-start.2 = (u32[32]{0:T(128)S(1)}, u32[32]{0:T(128)}, u32[]{:S(2)}) copy-start(u32[32]{0:T(128)} %constant.7) | copy-start | bytes 388
  83.5 5.1 %collective-permute-start.1 = (f32[12,3584]{1,0:T(8,128)S(1)}, f32[12,3584]{1,0:T(8,128)S(1)}, u32[]{:S(2)}, u32[]{:S(2)}) collective-permute-start(f32[12,3584]{1,0:T(8,128)S(1)} %slice.19), channel_id=1, source_target_pairs={{0,4},{4,8},{8,12},{1,5},{5,9},{9,13},{2,6},{6,10},{10,14},{3,7},{... | collective-permute-start | bytes 516104
  180.3 43.5 %collective-permute-start.2 = (f32[12,1024]{1,0:T(8,128)S(1)}, f32[12,1024]{1,0:T(8,128)S(1)}, u32[]{:S(2)}, u32[]{:S(2)}) collective-permute-start(f32[12,1024]{1,0:T(8,128)S(1)} %slice.20), channel_id=1, source_target_pairs={{0,1},{1,2},{2,3},{4,5},{5,6},{6,7},{8,9},{9,10},{10,11},{12,13},{... | collective-permute-start | bytes 147464
  181.8 42.8 %collective-permute-start = (f32[12,1024]{1,0:T(8,128)S(1)}, f32[12,1024]{1,0:T(8,128)S(1)}, u32[]{:S(2)}, u32[]{:S(2)}) collective-permute-start(f32[12,1024]{1,0:T(8,128)S(1)} %slice.18), channel_id=1, source_target_pairs={{0,1},{1,2},{2,3},{4,5},{5,6},{6,7},{8,9},{9,10},{10,11},{12,13},{... | collective-permute-start | bytes 147464
Sparse Core Ops, SparseCore 0:
  45.2 59.8 all-reduce.9
where the time goes:
time: 233 us; the launch traced here: 232 us
  blocking collectives  95.8 us (41%)
  matrix products  45.7 us (20%)
  local copies, waits for them, and re-layouts  35.4 us (15%)
  other arithmetic  17.8 us (8%)
  between operations  16.8 us (7%)
  waiting for transfers between devices  16.1 us (7%)
  starting transfers between devices  4.69 us (2%)
    unnamed x2, blocking collectives  40.5 us
    unnamed x25, local copies, waits for them, and re-layouts  28.8 us
    dot_general x2, matrix products, contract_first(): lax.dot_general(left, right, (((0,), (0,)), ((), ())), preferred_element_...  16.8 us
    unnamed x5, waiting for transfers between devices  16.1 us
    all_gather x1, blocking collectives, local(): tokens_all = lax.all_gather(tokens, 'col', axis=0, tiled=True)  15.5 us
    dot_general x2, matrix products, contract_last(): lax.dot_general(left, right, (((1,), (1,)), ((), ())), preferred_element_...  15.2 us
    convert_element_type x1, other arithmetic, local(): step_up = (factor * weight_grads[:, hidden_width:]).astype(jnp.bfloat16)  15.1 us
    all_gather x1, blocking collectives, local(): cotangent_all = lax.all_gather(cotangent, 'col', axis=0, tiled=True)  14 us
  transfers between devices with their start and end apart: 4, of which 1 were waited for; matrix products, arithmetic and copies ran while one was open for 29% of the time, Pallas kernels for 0%

commit v1 on v0

v1 whole, which is shorter than its diff:
```python
import functools

import jax
import jax.numpy as jnp
from jax import lax
from jax.experimental import pallas as pl
from jax.experimental.pallas import tpu as pltpu
from jax.sharding import PartitionSpec as P

MESH = pl.DeviceIdType.MESH
VMEM_BYTES = 60 * 1024 * 1024


def contract(left, right, dims):
    return lax.dot_general(left, right, ((dims[:1], dims[1:]), ((), ())), preferred_element_type=jnp.float32)


def layer_kernel(
    n_row, n_col, chunks,
    tok_ref, cot_ref, wg_hbm, wu_hbm, wd_hbm,
    *refs,
):
    outs, scratch = refs[: 6 + n_col - 1], refs[6 + n_col - 1 :]
    tok_mat, cot_mat, hid_ref, bg_ref, bu_ref, own_ref = outs[:6]
    send_refs = outs[6:]
    (wg, wu, wd, gathered, stage, part, d2d, xs, xr, act, acc, zacc,
     wsem, zsend, zrecv, dsend, drecv, xsend, xrecv, asend, arecv) = scratch
    rows = tok_ref.shape[0]
    half = rows * n_col // 2
    width = wg.shape[2]
    n_x = n_row // 2
    row, col = lax.axis_index("row"), lax.axis_index("col")
    core, x = lax.rem(row, 2), row // 2
    other = 1 - core
    core_peer = {"row": x * 2 + other}

    def weight_copies(k):
        static = isinstance(k, int) or chunks == 1
        start = (0 if chunks == 1 else k * width) if static else pl.multiple_of(k * width, width)
        cut = pl.ds(start, width)
        return (
            pltpu.make_async_copy(wg_hbm.at[:, cut], wg.at[k], wsem.at[0, k]),
            pltpu.make_async_copy(wu_hbm.at[:, cut], wu.at[k], wsem.at[1, k]),
            pltpu.make_async_copy(wd_hbm.at[cut, :], wd.at[k], wsem.at[2, k]),
        )

    for k in range(chunks):
        for copy in weight_copies(k):
            copy.start()

    barrier = pltpu.get_barrier_semaphore()
    peers = [core_peer]
    peers += [{"row": lax.rem(x + o, n_x) * 2 + core} for o in range(1, n_x)]
    peers += [{"col": lax.rem(col + o, n_col)} for o in range(1, n_col)]
    for peer in peers:
        pl.semaphore_signal(barrier, inc=1, device_id=peer, device_id_type=MESH)
    pl.semaphore_wait(barrier, len(peers))

    def gather_copy(t, o, slot):
        return pltpu.make_async_remote_copy(
            src_ref=(tok_ref, cot_ref)[t], dst_ref=gathered.at[t, slot],
            send_sem=zsend.at[t, o], recv_sem=zrecv.at[t, o],
            device_id={"col": lax.rem(col + o, n_col)}, device_id_type=MESH,
        )

    for t in range(2):
        for o in range(1, n_col):
            gather_copy(t, o, col).start()
    gathered[0, col] = tok_ref[...]
    gathered[1, col] = cot_ref[...]
    for t in range(2):
        for o in range(1, n_col):
            gather_copy(t, o, lax.rem(col + n_col - o, n_col)).wait_recv()
        for j in range(n_col):
            stage[j * rows : (j + 1) * rows, :] = gathered[t, j].astype(jnp.float32)
        (tok_mat, cot_mat)[t][...] = stage[...].astype(jnp.bfloat16)

    def core_copy(k):
        return pltpu.make_async_remote_copy(
            src_ref=part.at[k, other], dst_ref=d2d.at[k],
            send_sem=dsend.at[k], recv_sem=drecv.at[k],
            device_id=core_peer, device_id_type=MESH,
        )

    def x_copy(k, o):
        return pltpu.make_async_remote_copy(
            src_ref=xs.at[k], dst_ref=xr.at[k, o - 1],
            send_sem=xsend.at[k, o - 1], recv_sem=xrecv.at[k, o - 1],
            device_id={"row": lax.rem(x + o, n_x) * 2 + core}, device_id_type=MESH,
        )

    def act_copy(k, which):
        return pltpu.make_async_remote_copy(
            src_ref=act.at[k, which], dst_ref=act.at[k, which],
            send_sem=asend.at[k], recv_sem=arecv.at[k],
            device_id=core_peer, device_id_type=MESH,
        )

    def first_loop(k, carry):
        @pl.when(k < chunks)
        def _():
            for copy in weight_copies(k):
                copy.wait()
            sums = (
                contract(tok_mat[...], wg[k], (1, 0)),
                contract(tok_mat[...], wu[k], (1, 0)),
                contract(cot_mat[...], wd[k], (1, 1)),
            )
            for m in range(3):
                for h in range(2):
                    part[k, h, m * half : (m + 1) * half, :] = sums[m][h * half : (h + 1) * half]
            core_copy(k).start()

        @pl.when(k > 0)
        def _():
            last = k - 1
            core_copy(last).wait_recv()
            total = part[last, core] + d2d[last]
            d2d[last] = total
            xs[last] = total.astype(jnp.bfloat16)
            for o in range(1, n_x):
                x_copy(last, o).start()

        return carry

    lax.fori_loop(0, chunks + 1, first_loop, 0)

    acc[...] = jnp.zeros_like(acc)

    def second_loop(k, carry):
        @pl.when(k < chunks)
        def _():
            total = d2d[k]
            for o in range(1, n_x):
                x_copy(k, o).wait_recv()
                total = total + xr[k, o - 1].astype(jnp.float32)
            gate_val, up_val, back_hidden = total[:half], total[half : 2 * half], total[2 * half :]
            gate_sig = jax.nn.sigmoid(gate_val)
            activation = gate_val * gate_sig
            hidden = activation * up_val
            back_gate = back_hidden * up_val * gate_sig * (1.0 + gate_val * (1.0 - gate_sig))
            back_up = back_hidden * activation
            act[k, core] = jnp.concatenate([hidden, back_gate, back_up], axis=0).astype(jnp.bfloat16)
            act_copy(k, core).start()

        @pl.when(k > 0)
        def _():
            last = k - 1
            act_copy(last, other).wait_recv()
            low = act[last, 0].astype(jnp.float32)
            high = act[last, 1].astype(jnp.float32)
            picked = [
                jnp.concatenate(
                    [low[m * half : (m + 1) * half], high[m * half : (m + 1) * half]], axis=0
                ).astype(jnp.bfloat16)
                for m in range(3)
            ]
            hid_ref[last], bg_ref[last], bu_ref[last] = picked
            acc[0] += contract(picked[0], wd[last], (1, 0))
            acc[1] += contract(picked[1], wg[last], (1, 1)) + contract(picked[2], wu[last], (1, 1))

        return carry

    lax.fori_loop(0, chunks + 1, second_loop, 0)

    for t in range(2):
        for j in range(n_col):
            zacc[t, j] = acc[t, j * rows : (j + 1) * rows, :]
    own_ref[...] = zacc[:, col]
    for o in range(1, n_col):
        send_refs[o - 1][...] = zacc[:, lax.rem(col + o, n_col)].astype(jnp.bfloat16)

    for t in range(2):
        for o in range(1, n_col):
            gather_copy(t, o, col).wait_send()

    def drain(k, carry):
        core_copy(k).wait_send()
        for o in range(1, n_x):
            x_copy(k, o).wait_send()
        act_copy(k, core).wait_send()
        return carry

    lax.fori_loop(0, chunks, drain, 0)


def layer_call(n_row, n_col, width, tokens, cotangent, w_gate, w_up, w_down):
    rows, depth = tokens.shape
    hidden_width = w_gate.shape[1]
    chunks = hidden_width // width
    total = rows * n_col
    half3 = 3 * total // 2
    n_x = n_row // 2
    bf16, f32 = jnp.bfloat16, jnp.float32
    vmem = pl.BlockSpec(memory_space=pltpu.VMEM)
    hbm = pl.BlockSpec(memory_space=pl.ANY)
    out_shape = [jax.ShapeDtypeStruct((total, depth), bf16)] * 2
    out_shape += [jax.ShapeDtypeStruct((chunks, total, width), bf16)] * 3
    out_shape += [jax.ShapeDtypeStruct((2, rows, depth), f32)]
    out_shape += [jax.ShapeDtypeStruct((2, rows, depth), bf16)] * (n_col - 1)
    sem = pltpu.SemaphoreType.DMA
    return pl.pallas_call(
        functools.partial(layer_kernel, n_row, n_col, chunks),
        out_shape=out_shape,
        in_specs=[vmem, vmem, hbm, hbm, hbm],
        out_specs=[vmem] * len(out_shape),
        scratch_shapes=[
            pltpu.VMEM((chunks, depth, width), bf16),
            pltpu.VMEM((chunks, depth, width), bf16),
            pltpu.VMEM((chunks, width, depth), bf16),
            pltpu.VMEM((2, n_col, rows, depth), bf16),
            pltpu.VMEM((total, depth), f32),
            pltpu.VMEM((chunks, 2, half3, width), f32),
            pltpu.VMEM((chunks, half3, width), f32),
            pltpu.VMEM((chunks, half3, width), bf16),
            pltpu.VMEM((chunks, max(n_x - 1, 1), half3, width), bf16),
            pltpu.VMEM((chunks, 2, half3, width), bf16),
            pltpu.VMEM((2, total, depth), f32),
            pltpu.VMEM((2, n_col, rows, depth), f32),
            sem((3, chunks)),
            sem((2, n_col)),
            sem((2, n_col)),
            sem((chunks,)),
            sem((chunks,)),
            sem((chunks, max(n_x - 1, 1))),
            sem((chunks, max(n_x - 1, 1))),
            sem((chunks,)),
            sem((chunks,)),
        ],
        compiler_params=pltpu.CompilerParams(
            collective_id=0, has_side_effects=True, vmem_limit_bytes=VMEM_BYTES
        ),
        cost_estimate=pl.CostEstimate(
            flops=12 * total * depth * hidden_width,
            bytes_accessed=6 * depth * hidden_width,
            transcendentals=total * hidden_width,
        ),
    )(tokens, cotangent, w_gate, w_up, w_down)


def step_kernel(rate_ref, tok_ref, cot_ref, hid_ref, bg_ref, bu_ref, sg_ref, su_ref, sd_ref):
    factor = -rate_ref[0]
    sg_ref[...] = (factor * contract(tok_ref[...], bg_ref[0], (0, 0))).astype(jnp.bfloat16)
    su_ref[...] = (factor * contract(tok_ref[...], bu_ref[0], (0, 0))).astype(jnp.bfloat16)
    sd_ref[...] = (factor * contract(hid_ref[0], cot_ref[...], (0, 0))).astype(jnp.bfloat16)


def step_call(step_rate, tok_mat, cot_mat, hid, bg, bu):
    chunks, total, width = hid.shape
    depth = tok_mat.shape[1]
    whole = pl.BlockSpec((total, depth), lambda k: (0, 0))
    piece = pl.BlockSpec((1, total, width), lambda k: (k, 0, 0))
    wide = pl.BlockSpec((depth, width), lambda k: (0, k))
    tall = pl.BlockSpec((width, depth), lambda k: (k, 0))
    bf16 = jnp.bfloat16
    return pl.pallas_call(
        step_kernel,
        grid=(chunks,),
        out_shape=[
            jax.ShapeDtypeStruct((depth, chunks * width), bf16),
            jax.ShapeDtypeStruct((depth, chunks * width), bf16),
            jax.ShapeDtypeStruct((chunks * width, depth), bf16),
        ],
        in_specs=[pl.BlockSpec(memory_space=pltpu.SMEM), whole, whole, piece, piece, piece],
        out_specs=[wide, wide, tall],
        compiler_params=pltpu.CompilerParams(vmem_limit_bytes=VMEM_BYTES // 2),
        cost_estimate=pl.CostEstimate(
            flops=6 * total * depth * chunks * width,
            bytes_accessed=6 * depth * chunks * width,
            transcendentals=0,
        ),
    )(step_rate, tok_mat, cot_mat, hid, bg, bu)


def local(n_row, n_col, tokens, w_gate, w_up, w_down, cotangent, step_rate):
    hidden_width = w_gate.shape[1]
    width = 512 if hidden_width % 512 == 0 else hidden_width
    tok_mat, cot_mat, hid, bg, bu, own, *sends = layer_call(
        n_row, n_col, width, tokens, cotangent, w_gate, w_up, w_down
    )
    arrived = [
        lax.ppermute(block, "col", [(i, (i + o) % n_col) for i in range(n_col)])
        for o, block in enumerate(sends, 1)
    ]
    step_gate, step_up, step_down = step_call(step_rate, tok_mat, cot_mat, hid, bg, bu)
    sums = own
    for block in arrived:
        sums = sums + block.astype(jnp.float32)
    out_rows = (tokens.astype(jnp.float32) + sums[0]).astype(jnp.bfloat16)
    grad_in = (cotangent.astype(jnp.float32) + sums[1]).astype(jnp.bfloat16)
    return (out_rows, grad_in, step_gate, step_up, step_down)


def solution(mesh):
    in_specs = (
        P(("sweep", "col"), "row"),
        P("row", "col"),
        P("row", "col"),
        P("col", "row"),
        P(("sweep", "col"), "row"),
        P("sweep"),
    )
    out_specs = (
        P(("sweep", "col"), "row"),
        P(("sweep", "col"), "row"),
        P(("sweep", "row"), "col"),
        P(("sweep", "row"), "col"),
        P(("sweep", "col"), "row"),
    )
    body = functools.partial(local, mesh.shape["row"], mesh.shape["col"])
    return jax.shard_map(body, mesh=mesh, in_specs=in_specs, out_specs=out_specs, check_vma=False)
```

time: 233 us -> 64.5 us (0.28)
  blocking collectives: 95.8 us -> 0 us
  Pallas kernels: 0 us -> 51.6 us
  matrix products: 45.7 us -> 0 us
  local copies, waits for them, and re-layouts: 35.4 us -> 5.01 us
  other arithmetic: 17.8 us -> 1.64 us
  waiting for transfers between devices: 16.1 us -> 0.01 us
  between operations: 16.8 us -> 1.35 us
    all_gather x5 -> x0, blocking collectives: 55.2 us -> none  [the longest x1 15.5 us: local(): tokens_all = lax.all_gather(tokens, 'col', axis=0, tiled=True)]
    pallas_call x0 -> x2, Pallas kernels: none -> 51.6 us  [the longest x1 42.2 us: layer_call(): pl.pallas_call(functools.partial(layer_kernel, n_row, n_col, chunks), out...]
    dot_general x6 -> x0, matrix products: 45.7 us -> none  [the longest x2 16.8 us: contract_first(): lax.dot_general(left, right, (((0,), (0,)), ((), ())), preferred_element_...]
    unnamed x2 -> x0, blocking collectives: 40.5 us -> none
    unnamed x25 -> x14, local copies, waits for them, and re-layouts: 28.8 us -> 5.01 us
    unnamed x5 -> x0, waiting for transfers between devices: 16.1 us -> none
    convert_element_type x3 -> x1, other arithmetic: 16.3 us -> 0.67 us  [local(): grad_in = (cotangent.astype(jnp.float32) + sums[1]).astype(jnp.bfloat16)]
    concatenate x2 -> x0, local copies, waits for them, and re-layouts: 6.58 us -> none  [the longest x1 6.54 us: local(): w_both = jnp.concatenate([w_gate, w_up], axis=1)]
  transfers between devices with their start and end apart: 4 -> 3, of which waited for: 1 -> 0; matrix products, arithmetic and copies ran while one was open for 29% -> 0% of each run, Pallas kernels for 0% -> 15%
where the time goes in v1:
time: 64.5 us; the launch traced here: 64.1 us
  Pallas kernels  51.6 us (80%)
  local copies, waits for them, and re-layouts  5.01 us (8%)
  starting transfers between devices  4.47 us (7%)
  other arithmetic  1.64 us (3%)
  between operations  1.35 us (2%)
    pallas_call x1, Pallas kernels, layer_call(): pl.pallas_call(functools.partial(layer_kernel, n_row, n_col, chunks), out...  42.2 us
    pallas_call x1, Pallas kernels, step_call(): pl.pallas_call(step_kernel, grid=(chunks,), out_shape=[jax.ShapeDtypeStru...  9.4 us
    unnamed x14, local copies, waits for them, and re-layouts  5.01 us
    ppermute x3, starting transfers between devices, local(): lax.ppermute(block, 'col', [(i, (i + o) % n_col) for i in range(n_col)])  4.47 us
  transfers between devices with their start and end apart: 3, of which 0 were waited for; matrix products, arithmetic and copies ran while one was open for 0% of the time, Pallas kernels for 15%

profile of v1, /device:TPU:0, one launch (start us, length us, event | category | flops | bytes accessed | tf_op | source)
XLA Modules:
  0.0 64.1 jit_solution(18251999217727013325)
XLA Ops:
  0.6 0.0 copy-start.6
  0.6 0.0 copy-start.5
  0.7 42.2 %shard_map.101 = (bf16[80,1024]{1,0:T(8,128)(2,1)}, bf16[80,1024]{1,0:T(8,128)(2,1)}, bf16[7,80,512]{2,1,0:T(8,128)(2,1)}, bf16[7,80,512]{2,1,0:T(8,128)(2,1)}, ...) custom-call(bf16[20,1024]{1,0:T(8,128)(2,1)} %tok_ref.1, ...), custom_call_target="tpu_custom_call" | custom-call | flops 3523215360 | bytes 22020096 | tf_op jit(solution)/shard_map/pallas_call | solution.py:202
  42.9 1.2 %collective-permute-start = (bf16[2,20,1024]{2,1,0:T(8,128)(2,1)}, bf16[2,20,1024]{2,1,0:T(8,128)(2,1)S(1)}, u32[]{:S(2)}, u32[]{:S(2)}) collective-permute-start(bf16[2,20,1024]{2,1,0:T(8,128)(2,1)} %get-tuple-element.18), channel_id=1, source_target_pairs={{0,1},{1,2},{2,3},{3,0},{4,5},{5,6},{6,7},{7,4},{8,9},{9,10},{10,1... | collective-permute-start | bytes 245768 | tf_op jit(solution)/shard_map/ppermute | solution.py:282
  44.1 2.3 %collective-permute-start.1 = (bf16[2,20,1024]{2,1,0:T(8,128)(2,1)}, bf16[2,20,1024]{2,1,0:T(8,128)(2,1)S(1)}, u32[]{:S(2)}, u32[]{:S(2)}) collective-permute-start(bf16[2,20,1024]{2,1,0:T(8,128)(2,1)} %get-tuple-element.19), channel_id=1, source_target_pairs={{0,2},{1,3},{2,0},{3,1},{4,6},{5,7},{6,4},{7,5},{8,10},{9,11},{10,... | collective-permute-start | bytes 245768 | tf_op jit(solution)/shard_map/ppermute | solution.py:282
  46.4 0.9 %collective-permute-start.2 = (bf16[2,20,1024]{2,1,0:T(8,128)(2,1)}, bf16[2,20,1024]{2,1,0:T(8,128)(2,1)S(1)}, u32[]{:S(2)}, u32[]{:S(2)}) collective-permute-start(bf16[2,20,1024]{2,1,0:T(8,128)(2,1)} %get-tuple-element.20), channel_id=1, source_target_pairs={{0,3},{1,0},{2,1},{3,2},{4,7},{5,4},{6,5},{7,6},{8,11},{9,8},{10,9... | collective-permute-start | bytes 245768 | tf_op jit(solution)/shard_map/ppermute | solution.py:282
  48.0 0.0 copy-start
  48.0 1.1 %copy-done = bf16[7,80,512]{2,1,0:T(8,128)(2,1)S(1)} copy-done((bf16[7,80,512]{2,1,0:T(8,128)(2,1)S(1)}, bf16[7,80,512]{2,1,0:T(8,128)(2,1)}, u32[]{:S(2)}) %copy-start) | copy-done | bytes 573464
  49.0 0.0 copy-start.1
  49.0 1.1 %copy-done.1 = bf16[7,80,512]{2,1,0:T(8,128)(2,1)S(1)} copy-done((bf16[7,80,512]{2,1,0:T(8,128)(2,1)S(1)}, bf16[7,80,512]{2,1,0:T(8,128)(2,1)}, u32[]{:S(2)}) %copy-start.1) | copy-done | bytes 573464
  50.1 0.0 copy-start.2
  50.1 1.1 %copy-done.2 = bf16[7,80,512]{2,1,0:T(8,128)(2,1)S(1)} copy-done((bf16[7,80,512]{2,1,0:T(8,128)(2,1)S(1)}, bf16[7,80,512]{2,1,0:T(8,128)(2,1)}, u32[]{:S(2)}) %copy-start.2) | copy-done | bytes 573464
  51.2 0.0 copy-start.3
  51.2 0.9 %copy-done.3 = bf16[80,1024]{1,0:T(8,128)(2,1)S(1)} copy-done((bf16[80,1024]{1,0:T(8,128)(2,1)S(1)}, bf16[80,1024]{1,0:T(8,128)(2,1)}, u32[]{:S(2)}) %copy-start.3) | copy-done | bytes 163864
  52.1 0.0 copy-start.4
  52.1 0.9 %copy-done.4 = bf16[80,1024]{1,0:T(8,128)(2,1)S(1)} copy-done((bf16[80,1024]{1,0:T(8,128)(2,1)S(1)}, bf16[80,1024]{1,0:T(8,128)(2,1)}, u32[]{:S(2)}) %copy-start.4) | copy-done | bytes 163864
  53.0 9.4 %shard_map.102 = (bf16[1024,3584]{1,0:T(8,128)(2,1)}, bf16[1024,3584]{1,0:T(8,128)(2,1)}, bf16[3584,1024]{1,0:T(8,128)(2,1)}) custom-call(f32[1]{0:T(128)S(6)} %copy.11.rate_ref, bf16[80,1024]{1,0:T(8,128)(2,1)S(1)} %copy-done.3, bf16[80,1024]{1,0:T(8,128)(2,1)S(1)} %copy-done.4, bf16[7,80,512]{2,1,0:T(8,128)(2,1)S(1)} %copy-done, ...), custom_call_target="tpu_custom_call" | custom-call | flops 1761607680 | bytes 22020096 | tf_op jit(solution)/shard_map/pallas_call | solution.py:256
  62.4 0.0 collective-permute-done
  62.4 0.0 collective-permute-done.1
  62.4 0.0 collective-permute-done.2
  62.4 1.0 %convert_add_fusion = f32[2,20,1024]{2,1,0:T(8,128)S(1)} fusion(bf16[2,20,1024]{2,1,0:T(8,128)(2,1)S(1)} %collective-permute-done.2, bf16[2,20,1024]{2,1,0:T(8,128)(2,1)S(1)} %collective-permute-done.1, f32[2,20,1024]{2,1,0:T(8,128)} %get-tuple-element.17, bf16[2,20,1024]{2,1,0:T(8,128)(2,1)S(1)} %collective-permute-done), kind=kLoop, calls=%fused_computation | loop fusion | flops 245760 | bytes 573440 | tf_op jit(solution)/shard_map/add | solution.py:288
  63.4 0.0 copy-done.6
  63.4 0.0 copy-done.5
  63.4 0.7 %fusion.1 = (bf16[20,1024]{1,0:T(8,128)(2,1)}, bf16[20,1024]{1,0:T(8,128)(2,1)}) fusion(f32[2,20,1024]{2,1,0:T(8,128)S(1)} %convert_add_fusion, bf16[20,1024]{1,0:T(8,128)(2,1)S(1)} %copy-done.6, bf16[20,1024]{1,0:T(8,128)(2,1)S(1)} %copy-done.5), kind=kLoop, calls=%fused_computation.3 | loop fusion | flops 122880 | bytes 327680 | tf_op jit(solution)/shard_map/convert_element_type | solution.py:290
Async XLA Ops:
  0.6 62.7 %copy-start.6 = (bf16[20,1024]{1,0:T(8,128)(2,1)S(1)}, bf16[20,1024]{1,0:T(8,128)(2,1)}, u32[]{:S(2)}) copy-start(bf16[20,1024]{1,0:T(8,128)(2,1)} %cot_ref.1) | copy-start | bytes 122884
  0.6 62.7 %copy-start.5 = (bf16[20,1024]{1,0:T(8,128)(2,1)S(1)}, bf16[20,1024]{1,0:T(8,128)(2,1)}, u32[]{:S(2)}) copy-start(bf16[20,1024]{1,0:T(8,128)(2,1)} %tok_ref.1) | copy-start | bytes 122884
  42.9 19.5 %collective-permute-start = (bf16[2,20,1024]{2,1,0:T(8,128)(2,1)}, bf16[2,20,1024]{2,1,0:T(8,128)(2,1)S(1)}, u32[]{:S(2)}, u32[]{:S(2)}) collective-permute-start(bf16[2,20,1024]{2,1,0:T(8,128)(2,1)} %get-tuple-element.18), channel_id=1, source_target_pairs={{0,1},{1,2},{2,3},{3,0},{4,5},{5,6},{6,7},{7,4},{8,9},{9,10},{10,1... | collective-permute-start | bytes 245768 | tf_op jit(solution)/shard_map/ppermute | solution.py:282
  44.1 18.3 %collective-permute-start.1 = (bf16[2,20,1024]{2,1,0:T(8,128)(2,1)}, bf16[2,20,1024]{2,1,0:T(8,128)(2,1)S(1)}, u32[]{:S(2)}, u32[]{:S(2)}) collective-permute-start(bf16[2,20,1024]{2,1,0:T(8,128)(2,1)} %get-tuple-element.19), channel_id=1, source_target_pairs={{0,2},{1,3},{2,0},{3,1},{4,6},{5,7},{6,4},{7,5},{8,10},{9,11},{10,... | collective-permute-start | bytes 245768 | tf_op jit(solution)/shard_map/ppermute | solution.py:282
  46.4 16.0 %collective-permute-start.2 = (bf16[2,20,1024]{2,1,0:T(8,128)(2,1)}, bf16[2,20,1024]{2,1,0:T(8,128)(2,1)S(1)}, u32[]{:S(2)}, u32[]{:S(2)}) collective-permute-start(bf16[2,20,1024]{2,1,0:T(8,128)(2,1)} %get-tuple-element.20), channel_id=1, source_target_pairs={{0,3},{1,0},{2,1},{3,2},{4,7},{5,4},{6,5},{7,6},{8,11},{9,8},{10,9... | collective-permute-start | bytes 245768 | tf_op jit(solution)/shard_map/ppermute | solution.py:282
  48.0 1.1 %copy-start = (bf16[7,80,512]{2,1,0:T(8,128)(2,1)S(1)}, bf16[7,80,512]{2,1,0:T(8,128)(2,1)}, u32[]{:S(2)}) copy-start(bf16[7,80,512]{2,1,0:T(8,128)(2,1)} %get-tuple-element.23.hid_ref) | copy-start | bytes 1720324
  49.0 1.1 %copy-start.1 = (bf16[7,80,512]{2,1,0:T(8,128)(2,1)S(1)}, bf16[7,80,512]{2,1,0:T(8,128)(2,1)}, u32[]{:S(2)}) copy-start(bf16[7,80,512]{2,1,0:T(8,128)(2,1)} %get-tuple-element.24.bg_ref) | copy-start | bytes 1720324
  50.1 1.1 %copy-start.2 = (bf16[7,80,512]{2,1,0:T(8,128)(2,1)S(1)}, bf16[7,80,512]{2,1,0:T(8,128)(2,1)}, u32[]{:S(2)}) copy-start(bf16[7,80,512]{2,1,0:T(8,128)(2,1)} %get-tuple-element.25.bu_ref) | copy-start | bytes 1720324
  51.2 0.9 %copy-start.3 = (bf16[80,1024]{1,0:T(8,128)(2,1)S(1)}, bf16[80,1024]{1,0:T(8,128)(2,1)}, u32[]{:S(2)}) copy-start(bf16[80,1024]{1,0:T(8,128)(2,1)} %get-tuple-element.21.tok_ref) | copy-start | bytes 491524
  52.1 0.9 %copy-start.4 = (bf16[80,1024]{1,0:T(8,128)(2,1)S(1)}, bf16[80,1024]{1,0:T(8,128)(2,1)}, u32[]{:S(2)}) copy-start(bf16[80,1024]{1,0:T(8,128)(2,1)} %get-tuple-element.22.cot_ref) | copy-start | bytes 491524

commit v2 on v1

v2 whole, which is shorter than its diff:
```python
import functools

import jax
import jax.numpy as jnp
from jax import lax
from jax.experimental import pallas as pl
from jax.experimental.pallas import tpu as pltpu
from jax.sharding import PartitionSpec as P

MESH = pl.DeviceIdType.MESH
LAYER_VMEM = 49 * 1024 * 1024
STEP_VMEM = 30 * 1024 * 1024


def contract(left, right, dims):
    return lax.dot_general(left, right, ((dims[:1], dims[1:]), ((), ())), preferred_element_type=jnp.float32)


def layer_kernel(
    n_row, n_col, chunks,
    tok_ref, cot_ref, wg_hbm, wu_hbm, wd_hbm,
    *refs,
):
    outs, scratch = refs[: 6 + n_col - 1], refs[6 + n_col - 1 :]
    tok_mat, cot_mat, hid_ref, bg_ref, bu_ref, own_ref = outs[:6]
    send_refs = outs[6:]
    (wg, wu, wd, gathered, stage, part, d2d, xs, xr, bpart, bd2d, bxs, bxr, act, bact, acc, zacc,
     wsem, zsend, zrecv, dsem, asem, xsend, xrecv) = scratch
    rows = tok_ref.shape[0]
    half = rows * n_col // 2
    width = wg.shape[2]
    n_x = n_row // 2
    row, col = lax.axis_index("row"), lax.axis_index("col")
    core, x = lax.rem(row, 2), row // 2
    other = 1 - core
    core_peer = {"row": x * 2 + other}

    def weight_copy(m, k):
        static = isinstance(k, int) or chunks == 1
        start = (0 if chunks == 1 else k * width) if static else pl.multiple_of(k * width, width)
        cut = pl.ds(start, width)
        source = (wg_hbm, wu_hbm, wd_hbm)[m]
        return pltpu.make_async_copy(
            source.at[cut, :] if m == 2 else source.at[:, cut], (wg, wu, wd)[m].at[k], wsem.at[m, k]
        )

    for k in range(chunks):
        weight_copy(0, k).start()
        weight_copy(1, k).start()
    for k in range(chunks):
        weight_copy(2, k).start()

    barrier = pltpu.get_barrier_semaphore()
    peers = [core_peer]
    peers += [{"row": lax.rem(x + o, n_x) * 2 + core} for o in range(1, n_x)]
    peers += [{"col": lax.rem(col + o, n_col)} for o in range(1, n_col)]
    for peer in peers:
        pl.semaphore_signal(barrier, inc=1, device_id=peer, device_id_type=MESH)
    pl.semaphore_wait(barrier, len(peers))

    def gather_copy(t, o, slot):
        return pltpu.make_async_remote_copy(
            src_ref=(tok_ref, cot_ref)[t], dst_ref=gathered.at[t, slot],
            send_sem=zsend.at[t, o], recv_sem=zrecv.at[t, o],
            device_id={"col": lax.rem(col + o, n_col)}, device_id_type=MESH,
        )

    for t in range(2):
        for o in range(1, n_col):
            gather_copy(t, o, col).start()
    gathered[0, col] = tok_ref[...]
    gathered[1, col] = cot_ref[...]

    def assemble(t):
        for o in range(1, n_col):
            gather_copy(t, o, lax.rem(col + n_col - o, n_col)).wait_recv()
        for j in range(n_col):
            stage[j * rows : (j + 1) * rows, :] = gathered[t, j].astype(jnp.float32)
        (tok_mat, cot_mat)[t][...] = stage[...].astype(jnp.bfloat16)

    sums_of = (part, bpart)
    landed_of = (d2d, bd2d)
    xs_of = (xs, bxs)
    xr_of = (xr, bxr)
    act_of = (act, bact)

    def core_copy(t, k):
        return pltpu.make_async_remote_copy(
            src_ref=sums_of[t].at[k, other], dst_ref=landed_of[t].at[k],
            send_sem=dsem.at[0, t, k], recv_sem=dsem.at[1, t, k],
            device_id=core_peer, device_id_type=MESH,
        )

    def x_copy(t, k, o):
        return pltpu.make_async_remote_copy(
            src_ref=xs_of[t].at[k], dst_ref=xr_of[t].at[k, o - 1],
            send_sem=xsend.at[t, k, o - 1], recv_sem=xrecv.at[t, k, o - 1],
            device_id={"row": lax.rem(x + o, n_x) * 2 + core}, device_id_type=MESH,
        )

    def act_copy(t, k, which):
        return pltpu.make_async_remote_copy(
            src_ref=act_of[t].at[k, which], dst_ref=act_of[t].at[k, which],
            send_sem=asem.at[0, t, k], recv_sem=asem.at[1, t, k],
            device_id=core_peer, device_id_type=MESH,
        )

    def share(t, k):
        core_copy(t, k).wait_recv()
        total = sums_of[t][k, core] + landed_of[t][k]
        landed_of[t][k] = total
        xs_of[t][k] = total.astype(jnp.bfloat16)
        for o in range(1, n_x):
            x_copy(t, k, o).start()

    def total_of(t, k):
        total = landed_of[t][k]
        for o in range(1, n_x):
            x_copy(t, k, o).wait_recv()
            total = total + xr_of[t][k, o - 1].astype(jnp.float32)
        return total

    def both(t, k, m):
        return jnp.concatenate(
            [act_of[t][k, h, m * half : (m + 1) * half, :].astype(jnp.float32) for h in range(2)], axis=0
        ).astype(jnp.bfloat16)

    def staged(begin, finish):
        def step(k, carry):
            @pl.when(k < chunks)
            def _():
                begin(k)

            @pl.when(k > 0)
            def _():
                finish(k - 1)

            return carry

        lax.fori_loop(0, chunks + 1, step, 0)

    def forward_sums(k):
        weight_copy(0, k).wait()
        weight_copy(1, k).wait()
        for m, w in enumerate((wg, wu)):
            sums = contract(tok_mat[...], w[k], (1, 0))
            for h in range(2):
                part[k, h, m * half : (m + 1) * half, :] = sums[h * half : (h + 1) * half]
        core_copy(0, k).start()

    def backward_sums(k):
        weight_copy(2, k).wait()
        sums = contract(cot_mat[...], wd[k], (1, 1))
        for h in range(2):
            bpart[k, h] = sums[h * half : (h + 1) * half]
        core_copy(1, k).start()

    def forward_act(k):
        total = total_of(0, k)
        d2d[k] = total
        gate_val, up_val = total[:half], total[half:]
        act[k, core] = (gate_val * jax.nn.sigmoid(gate_val) * up_val).astype(jnp.bfloat16)
        act_copy(0, k, core).start()

    def forward_out(k):
        act_copy(0, k, other).wait_recv()
        hidden = both(0, k, 0)
        hid_ref[k] = hidden
        acc[0] += contract(hidden, wd[k], (1, 0))

    def backward_act(k):
        back_hidden = total_of(1, k)
        gate_val, up_val = d2d[k, :half], d2d[k, half:]
        gate_sig = jax.nn.sigmoid(gate_val)
        back_gate = back_hidden * up_val * gate_sig * (1.0 + gate_val * (1.0 - gate_sig))
        back_up = back_hidden * (gate_val * gate_sig)
        bact[k, core] = jnp.concatenate([back_gate, back_up], axis=0).astype(jnp.bfloat16)
        act_copy(1, k, core).start()

    def backward_out(k):
        act_copy(1, k, other).wait_recv()
        back_gate, back_up = both(1, k, 0), both(1, k, 1)
        bg_ref[k], bu_ref[k] = back_gate, back_up
        acc[1] += contract(back_gate, wg[k], (1, 1)) + contract(back_up, wu[k], (1, 1))

    acc[...] = jnp.zeros_like(acc)
    assemble(0)
    staged(forward_sums, lambda k: share(0, k))
    assemble(1)
    staged(backward_sums, lambda k: share(1, k))
    staged(forward_act, forward_out)
    staged(backward_act, backward_out)

    for t in range(2):
        for j in range(n_col):
            zacc[t, j] = acc[t, j * rows : (j + 1) * rows, :]
    own_ref[...] = zacc[:, col]
    for o in range(1, n_col):
        send_refs[o - 1][...] = zacc[:, lax.rem(col + o, n_col)].astype(jnp.bfloat16)

    for t in range(2):
        for o in range(1, n_col):
            gather_copy(t, o, col).wait_send()

    def drain(k, carry):
        for t in range(2):
            core_copy(t, k).wait_send()
            for o in range(1, n_x):
                x_copy(t, k, o).wait_send()
            act_copy(t, k, core).wait_send()
        return carry

    lax.fori_loop(0, chunks, drain, 0)


def layer_call(n_row, n_col, width, tokens, cotangent, w_gate, w_up, w_down):
    rows, depth = tokens.shape
    hidden_width = w_gate.shape[1]
    chunks = hidden_width // width
    total = rows * n_col
    half = total // 2
    others = max(n_row // 2 - 1, 1)
    bf16, f32 = jnp.bfloat16, jnp.float32
    vmem = pl.BlockSpec(memory_space=pltpu.VMEM)
    hbm = pl.BlockSpec(memory_space=pl.ANY)
    out_shape = [jax.ShapeDtypeStruct((total, depth), bf16)] * 2
    out_shape += [jax.ShapeDtypeStruct((chunks, total, width), bf16)] * 3
    out_shape += [jax.ShapeDtypeStruct((2, rows, depth), f32)]
    out_shape += [jax.ShapeDtypeStruct((2, rows, depth), bf16)] * (n_col - 1)
    sem = pltpu.SemaphoreType.DMA
    return pl.pallas_call(
        functools.partial(layer_kernel, n_row, n_col, chunks),
        out_shape=out_shape,
        in_specs=[vmem, vmem, hbm, hbm, hbm],
        out_specs=[vmem] * len(out_shape),
        scratch_shapes=[
            pltpu.VMEM((chunks, depth, width), bf16),
            pltpu.VMEM((chunks, depth, width), bf16),
            pltpu.VMEM((chunks, width, depth), bf16),
            pltpu.VMEM((2, n_col, rows, depth), bf16),
            pltpu.VMEM((total, depth), f32),
            pltpu.VMEM((chunks, 2, total, width), f32),
            pltpu.VMEM((chunks, total, width), f32),
            pltpu.VMEM((chunks, total, width), bf16),
            pltpu.VMEM((chunks, others, total, width), bf16),
            pltpu.VMEM((chunks, 2, half, width), f32),
            pltpu.VMEM((chunks, half, width), f32),
            pltpu.VMEM((chunks, half, width), bf16),
            pltpu.VMEM((chunks, others, half, width), bf16),
            pltpu.VMEM((chunks, 2, half, width), bf16),
            pltpu.VMEM((chunks, 2, total, width), bf16),
            pltpu.VMEM((2, total, depth), f32),
            pltpu.VMEM((2, n_col, rows, depth), f32),
            sem((3, chunks)),
            sem((2, n_col)),
            sem((2, n_col)),
            sem((2, 2, chunks)),
            sem((2, 2, chunks)),
            sem((2, chunks, others)),
            sem((2, chunks, others)),
        ],
        compiler_params=pltpu.CompilerParams(
            collective_id=0, has_side_effects=True, vmem_limit_bytes=LAYER_VMEM
        ),
        cost_estimate=pl.CostEstimate(
            flops=12 * total * depth * hidden_width,
            bytes_accessed=6 * depth * hidden_width,
            transcendentals=total * hidden_width,
        ),
    )(tokens, cotangent, w_gate, w_up, w_down)


def step_kernel(rate_ref, tok_ref, cot_ref, hid_ref, bg_ref, bu_ref, sg_ref, su_ref, sd_ref):
    factor = -rate_ref[0]
    sg_ref[...] = (factor * contract(tok_ref[...], bg_ref[0], (0, 0))).astype(jnp.bfloat16)
    su_ref[...] = (factor * contract(tok_ref[...], bu_ref[0], (0, 0))).astype(jnp.bfloat16)
    sd_ref[...] = (factor * contract(hid_ref[0], cot_ref[...], (0, 0))).astype(jnp.bfloat16)


def step_call(step_rate, tok_mat, cot_mat, hid, bg, bu):
    chunks, total, width = hid.shape
    depth = tok_mat.shape[1]
    whole = pl.BlockSpec((total, depth), lambda k: (0, 0))
    piece = pl.BlockSpec((1, total, width), lambda k: (k, 0, 0))
    wide = pl.BlockSpec((depth, width), lambda k: (0, k))
    tall = pl.BlockSpec((width, depth), lambda k: (k, 0))
    bf16 = jnp.bfloat16
    return pl.pallas_call(
        step_kernel,
        grid=(chunks,),
        out_shape=[
            jax.ShapeDtypeStruct((depth, chunks * width), bf16),
            jax.ShapeDtypeStruct((depth, chunks * width), bf16),
            jax.ShapeDtypeStruct((chunks * width, depth), bf16),
        ],
        in_specs=[pl.BlockSpec(memory_space=pltpu.SMEM), whole, whole, piece, piece, piece],
        out_specs=[wide, wide, tall],
        compiler_params=pltpu.CompilerParams(vmem_limit_bytes=STEP_VMEM),
        cost_estimate=pl.CostEstimate(
            flops=6 * total * depth * chunks * width,
            bytes_accessed=6 * depth * chunks * width,
            transcendentals=0,
        ),
    )(step_rate, tok_mat, cot_mat, hid, bg, bu)


def local(n_row, n_col, tokens, w_gate, w_up, w_down, cotangent, step_rate):
    hidden_width = w_gate.shape[1]
    width = 512 if hidden_width % 512 == 0 else hidden_width
    tok_mat, cot_mat, hid, bg, bu, own, *sends = layer_call(
        n_row, n_col, width, tokens, cotangent, w_gate, w_up, w_down
    )
    arrived = [
        lax.ppermute(block, "col", [(i, (i + o) % n_col) for i in range(n_col)])
        for o, block in enumerate(sends, 1)
    ]
    step_gate, step_up, step_down = step_call(step_rate, tok_mat, cot_mat, hid, bg, bu)
    finished = []
    for t, kept in enumerate((tokens, cotangent)):
        sums = own[t]
        for block in arrived:
            sums = sums + block[t].astype(jnp.float32)
        finished.append((kept.astype(jnp.float32) + sums).astype(jnp.bfloat16))
    out_rows, grad_in = finished
    return (out_rows, grad_in, step_gate, step_up, step_down)


def solution(mesh):
    in_specs = (
        P(("sweep", "col"), "row"),
        P("row", "col"),
        P("row", "col"),
        P("col", "row"),
        P(("sweep", "col"), "row"),
        P("sweep"),
    )
    out_specs = (
        P(("sweep", "col"), "row"),
        P(("sweep", "col"), "row"),
        P(("sweep", "row"), "col"),
        P(("sweep", "row"), "col"),
        P(("sweep", "col"), "row"),
    )
    body = functools.partial(local, mesh.shape["row"], mesh.shape["col"])
    return jax.shard_map(body, mesh=mesh, in_specs=in_specs, out_specs=out_specs, check_vma=False)
```

time: 64.5 us -> 56.1 us (0.87)
  Pallas kernels: 51.6 us -> 47.2 us
  local copies, waits for them, and re-layouts: 5.01 us -> 1.59 us
  other arithmetic: 1.64 us -> 0.7 us
  starting transfers between devices: 4.47 us -> 5.15 us
    pallas_call x1, Pallas kernels: 42.2 us -> 37.7 us  [layer_call(): pl.pallas_call(functools.partial(layer_kernel, n_row, n_col, chunks), out...]
    unnamed x14 -> x4, local copies, waits for them, and re-layouts: 5.01 us -> 1.59 us
    add x1 -> x0, other arithmetic: 0.97 us -> none  [local(): sums = sums + block.astype(jnp.float32)]
    ppermute x3, starting transfers between devices: 4.47 us -> 5.15 us  [local(): lax.ppermute(block, 'col', [(i, (i + o) % n_col) for i in range(n_col)])]
  transfers between devices with their start and end apart: 3 -> 3, of which waited for: 0 -> 0; matrix products, arithmetic and copies ran while one was open for 0% -> 0% of each run, Pallas kernels for 15% -> 17%
where the time goes in v2:
time: 56.1 us; the launch traced here: 55.9 us
  Pallas kernels  47.2 us (84%)
  starting transfers between devices  5.15 us (9%)
  local copies, waits for them, and re-layouts  1.59 us (3%)
  between operations  1.31 us (2%)
  other arithmetic  0.7 us (1%)
    pallas_call x1, Pallas kernels, layer_call(): pl.pallas_call(functools.partial(layer_kernel, n_row, n_col, chunks), out...  37.7 us
    pallas_call x1, Pallas kernels, step_call(): pl.pallas_call(step_kernel, grid=(chunks,), out_shape=[jax.ShapeDtypeStru...  9.42 us
    ppermute x3, starting transfers between devices, local(): lax.ppermute(block, 'col', [(i, (i + o) % n_col) for i in range(n_col)])  5.15 us
    unnamed x4, local copies, waits for them, and re-layouts  1.59 us
  transfers between devices with their start and end apart: 3, of which 0 were waited for; matrix products, arithmetic and copies ran while one was open for 0% of the time, Pallas kernels for 17%

profile of v2, /device:TPU:0, one launch (start us, length us, event | category | flops | bytes accessed | tf_op | source)
XLA Modules:
  0.0 55.9 jit_solution(15181338737513301273)
XLA Ops:
  0.6 0.0 copy-start
  0.6 0.8 %copy-done = bf16[20,1024]{1,0:T(8,128)(2,1)S(1)} copy-done((bf16[20,1024]{1,0:T(8,128)(2,1)S(1)}, bf16[20,1024]{1,0:T(8,128)(2,1)}, u32[]{:S(2)}) %copy-start) | copy-done | bytes 40984
  1.4 0.0 copy-start.1
  1.4 0.8 %copy-done.1 = bf16[20,1024]{1,0:T(8,128)(2,1)S(1)} copy-done((bf16[20,1024]{1,0:T(8,128)(2,1)S(1)}, bf16[20,1024]{1,0:T(8,128)(2,1)}, u32[]{:S(2)}) %copy-start.1) | copy-done | bytes 40984
  2.2 37.7 %shard_map.101 = (bf16[80,1024]{1,0:T(8,128)(2,1)S(1)}, bf16[80,1024]{1,0:T(8,128)(2,1)S(1)}, bf16[7,80,512]{2,1,0:T(8,128)(2,1)S(1)}, bf16[7,80,512]{2,1,0:T(8,...) custom-call(bf16[20,1024]{1,0:T(8,128)(2,1)S(1)} %copy-done, ...), custom_call_target="tpu_custom_call" | custom-call | flops 3523215360 | bytes 22020096 | tf_op jit(solution)/shard_map/pallas_call | solution.py:231
  40.0 2.7 %collective-permute-start = (bf16[2,20,1024]{2,1,0:T(8,128)(2,1)S(1)}, bf16[2,20,1024]{2,1,0:T(8,128)(2,1)S(1)}, u32[]{:S(2)}, u32[]{:S(2)}) collective-permute-start(bf16[2,20,1024]{2,1,0:T(8,128)(2,1)S(1)} %get-tuple-element.18), channel_id=1, source_target_pairs={{0,1},{1,2},{2,3},{3,0},{4,5},{5,6},{6,7},{7,4},{8,9},{9,10},{10,1... | collective-permute-start | bytes 245768 | tf_op jit(solution)/shard_map/ppermute | solution.py:314
  42.7 2.4 %collective-permute-start.1 = (bf16[2,20,1024]{2,1,0:T(8,128)(2,1)S(1)}, bf16[2,20,1024]{2,1,0:T(8,128)(2,1)S(1)}, u32[]{:S(2)}, u32[]{:S(2)}) collective-permute-start(bf16[2,20,1024]{2,1,0:T(8,128)(2,1)S(1)} %get-tuple-element.19), channel_id=1, source_target_pairs={{0,2},{1,3},{2,0},{3,1},{4,6},{5,7},{6,4},{7,5},{8,10},{9,11},{10,... | collective-permute-start | bytes 245768 | tf_op jit(solution)/shard_map/ppermute | solution.py:314
  45.1 0.0 collective-permute-start.2
  45.8 9.4 %shard_map.102 = (bf16[1024,3584]{1,0:T(8,128)(2,1)}, bf16[1024,3584]{1,0:T(8,128)(2,1)}, bf16[3584,1024]{1,0:T(8,128)(2,1)}) custom-call(f32[1]{0:T(128)S(6)} %copy.11.rate_ref, bf16[80,1024]{1,0:T(8,128)(2,1)S(1)} %get-tuple-element.21.tok_ref, bf16[80,1024]{1,0:T(8,128)(2,1)S(1)} %get-tuple-element.22.cot_ref, ...), custom_call_target="tpu_custom_call" | custom-call | flops 1761607680 | bytes 22020096 | tf_op jit(solution)/shard_map/pallas_call | solution.py:288
  55.2 0.0 collective-permute-done
  55.2 0.0 collective-permute-done.1
  55.2 0.0 collective-permute-done.2
  55.2 0.7 %fusion = (bf16[20,1024]{1,0:T(8,128)(2,1)}, bf16[20,1024]{1,0:T(8,128)(2,1)}) fusion(f32[2,20,1024]{2,1,0:T(8,128)S(1)} %get-tuple-element.17, bf16[20,1024]{1,0:T(8,128)(2,1)S(1)} %copy-done.1, bf16[2,20,1024]{2,1,0:T(8,128)(2,1)S(1)} %collective-permute-done.2, bf16[2,20,1024]{2,1,0:T(8,128)(2,1)S(1)} %collective-permute-done.1, ...), kind=kLoop, calls=%fused_computation.1 | loop fusion | flops 368640 | bytes 573440 | tf_op jit(solution)/shard_map/convert_element_type | solution.py:323
Async XLA Ops:
  0.6 0.8 %copy-start = (bf16[20,1024]{1,0:T(8,128)(2,1)S(1)}, bf16[20,1024]{1,0:T(8,128)(2,1)}, u32[]{:S(2)}) copy-start(bf16[20,1024]{1,0:T(8,128)(2,1)} %tok_ref.1) | copy-start | bytes 122884
  1.4 0.8 %copy-start.1 = (bf16[20,1024]{1,0:T(8,128)(2,1)S(1)}, bf16[20,1024]{1,0:T(8,128)(2,1)}, u32[]{:S(2)}) copy-start(bf16[20,1024]{1,0:T(8,128)(2,1)} %cot_ref.1) | copy-start | bytes 122884
  40.0 15.2 %collective-permute-start = (bf16[2,20,1024]{2,1,0:T(8,128)(2,1)S(1)}, bf16[2,20,1024]{2,1,0:T(8,128)(2,1)S(1)}, u32[]{:S(2)}, u32[]{:S(2)}) collective-permute-start(bf16[2,20,1024]{2,1,0:T(8,128)(2,1)S(1)} %get-tuple-element.18), channel_id=1, source_target_pairs={{0,1},{1,2},{2,3},{3,0},{4,5},{5,6},{6,7},{7,4},{8,9},{9,10},{10,1... | collective-permute-start | bytes 245768 | tf_op jit(solution)/shard_map/ppermute | solution.py:314
  42.7 12.5 %collective-permute-start.1 = (bf16[2,20,1024]{2,1,0:T(8,128)(2,1)S(1)}, bf16[2,20,1024]{2,1,0:T(8,128)(2,1)S(1)}, u32[]{:S(2)}, u32[]{:S(2)}) collective-permute-start(bf16[2,20,1024]{2,1,0:T(8,128)(2,1)S(1)} %get-tuple-element.19), channel_id=1, source_target_pairs={{0,2},{1,3},{2,0},{3,1},{4,6},{5,7},{6,4},{7,5},{8,10},{9,11},{10,... | collective-permute-start | bytes 245768 | tf_op jit(solution)/shard_map/ppermute | solution.py:314
  45.1 10.1 %collective-permute-start.2 = (bf16[2,20,1024]{2,1,0:T(8,128)(2,1)S(1)}, bf16[2,20,1024]{2,1,0:T(8,128)(2,1)S(1)}, u32[]{:S(2)}, u32[]{:S(2)}) collective-permute-start(bf16[2,20,1024]{2,1,0:T(8,128)(2,1)S(1)} %get-tuple-element.20), channel_id=1, source_target_pairs={{0,3},{1,0},{2,1},{3,2},{4,7},{5,4},{6,5},{7,6},{8,11},{9,8},{10,9... | collective-permute-start | bytes 245768 | tf_op jit(solution)/shard_map/ppermute | solution.py:314
